TPU v7x, 256 devices: a whole 4x4x8 slice. The times are simulated.
256 devices in a mesh: dp: 16 (over y_hi, x, core), seq: 16 (over y_lo, z).
Axes of the slice: x: 4, y: 4 (y_hi: 2, y_lo: 2; y = y_hi * 2 + y_lo), z: 8, core: 2. Of those that a mesh axis runs over, the one named last changes fastest.
Arguments:
- tokens: bfloat16 [16, 4096, 1280], P('dp', 'seq'), may hold values from -6 to 6
- tube_index: int32 [16, 4096], P('dp', 'seq'), may hold values from 0 to 16383
- counts: int32 [16, 16], P('dp', 'seq'), may hold values from 128 to 256
- qkv_weight: bfloat16 [1280, 3840], P('dp'), may hold values from -4 to 4
- proj_weight: bfloat16 [1280, 1280], P('dp'), may hold values from -0.15625 to 0.15625
- ctx_b: bfloat16 [16, 4096, 1280], P('dp', 'seq'), may hold values from -12 to 12
- cot_b: bfloat16 [16, 4096, 1280], P('dp', 'seq'), may hold values from -12 to 12
- b_counts: int32 [16, 16], P('dp', 'seq'), may hold values from 128 to 256
Outputs:
- out_a: bfloat16 [16, 4096, 1280], P('dp', 'seq')
- weight_grad: float32 [1280, 1280], P('dp')
Inputs may be any that keep to these rules, and one draw needn't show every extreme that they name: `counts`: slots of a device's block past its count hold padding. `b_counts`: slots of a device's block past its count hold padding.
All inputs are finite; a program needn't handle non-finite values.
Results may differ from a plain program's by a relative error of at most 0.017.
Values may be sent and summed in bfloat16 or wider, within the bound.
No kernel may reach another device: no remote copies, remote signals or barrier semaphores. Data moves between devices by JAX's collectives and lax.ppermute only.
A program may use at most 128 MiB of HBM per device.

v0:
```python
import math

import jax
import jax.numpy as jnp
from jax import lax
from jax.sharding import Mesh
from jax.sharding import PartitionSpec as P

HEADS = 16
SEQ = ("seq_0", "seq_1")
DP = ("dp_0", "dp_1", "dp_2")


def in_order(parts, dim):
    shape = list(parts.shape[1:])
    shape[dim] *= parts.shape[0]
    return jnp.moveaxis(parts, 0, dim).reshape(shape)


def stacked_from(x, axes, sequence):
    parts = x
    for k in sequence:
        parts = lax.all_gather(parts, axes[k])
    done = sequence[::-1]
    back = [done.index(k) for k in range(len(axes))]
    parts = parts.transpose(*back, *range(len(axes), parts.ndim))
    return parts.reshape(-1, *x.shape)


def gathered_by_axis(x, axes, sequence, dim):
    return in_order(stacked_from(x, axes, sequence), dim)


def over_pieces(x, axis):
    return lax.all_gather(x, axis).astype(jnp.float32).sum(0)


def embed(tube_ids, model_width):
    half_width = model_width // 2
    positions = jnp.arange(half_width, dtype=jnp.float32)
    frequency = jnp.exp(positions * (-2.0 * math.log(10000.0) / model_width))
    angles = tube_ids.astype(jnp.float32)[:, None] * frequency[None, :]
    return jnp.concatenate([jnp.sin(angles), jnp.cos(angles)], axis=1)


def layer_norm(values):
    centered = values - jnp.mean(values, axis=1, keepdims=True)
    spread = jnp.mean(centered * centered, axis=1, keepdims=True)
    return centered * lax.rsqrt(spread + 1e-06)


def attend(grouped, valid_keys, heads_here, head_width):
    seq_length = grouped.shape[0]
    query_rows = grouped[:, 0].reshape(seq_length, heads_here, head_width)
    key_rows = grouped[:, 1].reshape(seq_length, heads_here, head_width)
    value_rows = grouped[:, 2].reshape(seq_length, heads_here, head_width)
    block_rows = math.gcd(seq_length, 512)
    score_scale = 1.0 / math.sqrt(head_width)
    blocked = query_rows.reshape(seq_length // block_rows, block_rows, heads_here, head_width)

    def one_block(block_query):
        scores = (
            jnp.einsum("qhd,khd->hqk", block_query, key_rows, preferred_element_type=jnp.float32)
            * score_scale
        )
        scores = jnp.where(valid_keys[None, None, :], scores, -1e30)
        top_score = jnp.max(scores, axis=2, keepdims=True)
        exponent = jnp.exp(scores - top_score)
        weights = (exponent / jnp.sum(exponent, axis=2, keepdims=True)).astype(jnp.bfloat16)
        return jnp.einsum(
            "hqk,khd->qhd", weights, value_rows, preferred_element_type=jnp.float32
        ).astype(jnp.bfloat16)

    return lax.map(one_block, blocked).reshape(seq_length, heads_here * head_width)


def on_device(tokens, tube_index, counts, qkv_weight, proj_weight, ctx_b, cot_b, b_counts):
    slot_cap = tokens.shape[1]
    model_width = tokens.shape[2]
    seq_count = lax.axis_size(SEQ)
    dp_count = lax.axis_size(DP)
    heads_here = HEADS // seq_count
    head_width = model_width // HEADS
    with_pos = tokens[0].astype(jnp.float32) + embed(tube_index[0], model_width)
    normed = layer_norm(with_pos).astype(jnp.bfloat16)
    columns = normed
    projected = jnp.dot(
        columns,
        lax.all_gather(qkv_weight, DP, axis=0, tiled=True),
        preferred_element_type=jnp.float32,
    ).astype(jnp.bfloat16)
    all_counts = gathered_by_axis(counts, SEQ, (0, 1), 1)
    slot_ids = lax.broadcasted_iota(jnp.int32, (1, slot_cap), 1)
    valid_keys = (slot_ids < all_counts[0][:, None]).reshape(seq_count * slot_cap)
    grouped = lax.all_to_all(
        projected.reshape(slot_cap, 3, model_width), SEQ, split_axis=2, concat_axis=0, tiled=True
    )
    head_context = attend(grouped, valid_keys, heads_here, head_width)
    context = lax.all_to_all(head_context, SEQ, split_axis=0, concat_axis=1, tiled=True)
    columns = context
    mixed = jnp.dot(
        columns, gathered_by_axis(proj_weight, DP, (0, 1, 2), 0), preferred_element_type=jnp.float32
    )
    out_a = (with_pos + mixed).astype(jnp.bfloat16)[None]
    row_ids = lax.broadcasted_iota(jnp.int32, (slot_cap, 1), 0)
    keep_rows = row_ids < b_counts[0, 0]
    masked_cot = jnp.where(keep_rows, cot_b[0], jnp.zeros((), jnp.bfloat16))
    factor = 1.0 / math.sqrt(dp_count * seq_count * slot_cap)
    column_part = ctx_b[0]
    own_rows = lax.psum_scatter(
        lax.dot_general(
            column_part, masked_cot, (((0,), (0,)), ((), ())), preferred_element_type=jnp.float32
        )
        * factor,
        DP,
        scatter_dimension=0,
        tiled=True,
    )
    weight_grad = over_pieces(own_rows.astype(jnp.bfloat16), SEQ).astype(jnp.float32)
    return (out_a, weight_grad)


def solution(mesh):
    split = Mesh(mesh.devices.reshape(2, 4, 2, 2, 8), ("dp_0", "dp_1", "dp_2", "seq_0", "seq_1"))
    return jax.shard_map(
        on_device,
        mesh=split,
        in_specs=(
            P(DP, SEQ, None),
            P(DP, SEQ),
            P(DP, SEQ),
            P(DP, None),
            P(DP, None),
            P(DP, SEQ, None),
            P(DP, SEQ, None),
            P(DP, SEQ),
        ),
        out_specs=(P(DP, SEQ, None), P(DP, None)),
        check_vma=False,
    )
```

profile of v0, /device:TPU:4, one launch (start us, length us, event | category | flops | bytes accessed | tf_op | source)
XLA Modules:
  0.0 355.5 jit_solution(13332053079246862315)
XLA Ops:
  7.2 0.7 all-gather.11.cloned.1.call-update
  8.0 10.9 %all-gather.2 = bf16[160,1280]{1,0:T(8,128)(2,1)} all-gather(bf16[80,1280]{1,0:T(8,128)(2,1)} %param.14), channel_id=4, replica_groups=mesh['dp_0'=2,'dp_1'=4,'dp_2'=2,'seq_0'=2,'seq_1'=8] {'dp_0'}, dimensions={0}, use_global_device_ids=true | all-gather | bytes 614400 | tf_op jit(solution)/shard_map/all_gather | solution.py:23
  19.6 5.0 %fusion.16 = f32[1280,1280]{0,1:T(8,128)} fusion(bf16[1,256,1280]{2,1,0:T(8,128)(2,1)S(1)} %copy-done, bf16[1,256,1280]{2,1,0:T(8,128)(2,1)} %param.16, pred[256]{0:T(512)(128)(4,1)S(1)} %iota_compare_fusion.1), kind=kOutput, calls=%fused_computation.20 | convolution fusion | flops 840826880 | bytes 7864576 | tf_op jit(solution)/shard_map/dot_general | solution.py:111
  24.6 8.3 %copy.45 = f32[1280,1280]{1,0:T(8,128)} copy(f32[1280,1280]{0,1:T(8,128)} %fusion.16) | data formatting | bytes 13107200
  32.9 0.7 copy-done.9
  33.5 2.3 multiply_sine_fusion
  35.9 0.2 fusion.27
  36.2 0.3 multiply_reduce_fusion
  36.5 59.3 %all-gather.11.cloned.1.call-done = bf16[1280,3840]{1,0:T(8,128)(2,1)} async-done(((bf16[80,3840]{1,0:T(8,128)(2,1)}), bf16[1280,3840]{1,0:T(8,128)(2,1)}) %all-gather.11.cloned.1.call-update) | async-done | bytes 9830416 | tf_op jit(solution)/shard_map/all_gather | solution.py:89
  95.8 7.9 %convolution_convert_fusion = bf16[256,3840]{1,0:T(8,128)(2,1)} fusion(bf16[1280,3840]{1,0:T(8,128)(2,1)} %all-gather.11.cloned.1.call-done, f32[256]{0:T(256)S(1)} %add_rsqrt_fusion, f32[256]{0:T(256)S(1)} %broadcast_multiply_fusion, f32[256,640]{1,0:T(8,128)S(1)} %get-tuple-element.86, f32[256,640]{1,0:T(8,128)S(1)} %get-tuple-element.85, ...), kind=kOutput, calls=%fused_computation.22 | convolution fusion | flops 2519531520 | bytes 13764608 | tf_op jit(solution)/shard_map/dot_general | solution.py:87
  103.6 2.7 copy.35
  106.3 11.2 %copy.36 = bf16[256,3,1280]{0,1,2:T(4,128)(2,1)} copy(bf16[256,3,1280]{0,2,1:T(8,128)(2,1)S(1)} %bitcast.93) | data formatting | bytes 3932160 | tf_op jit(solution)/shard_map/reshape | solution.py:96
  117.6 7.3 %all-to-all-start = ((bf16[256,3,1280]{0,1,2:T(4,128)(2,1)}), bf16[256,3,1280]{0,1,2:T(4,128)(2,1)S(1)}, u32[]{:S(2)}, u32[]{:S(2)}) async-start(bf16[256,3,1280]{0,1,2:T(4,128)(2,1)} %copy.36), calls=%async_computation | async-start | bytes 5242880 | tf_op jit(solution)/shard_map/all_to_all | solution.py:95
  124.9 0.3 all-gather.13.cloned.1.call-done
  125.2 0.2 all-gather.15.cloned.1.call-update
  126.1 0.6 dynamic-slice
  126.7 0.9 bitcast_dynamic-update-slice_fusion
  127.6 4.5 %all-reduce = s32[2]{0:T(128)S(1)} all-reduce(s32[2]{0:T(128)S(1)} %bitcast_dynamic-update-slice_fusion), channel_id=2, replica_groups=mesh['dp_0'=2,'dp_1'=4,'dp_2'=2,'seq_0'=2,'seq_1'=8] {'seq_0'}, use_global_device_ids=true, to_apply=%add | all-reduce | flops 2 | bytes 16
  132.1 0.6 dynamic-slice.1
  133.3 0.2 dynamic-update-slice.1
  133.6 61.1 %all-reduce.1 = s32[16]{0:T(128)S(1)} all-reduce(s32[16]{0:T(128)S(1)} %dynamic-update-slice.1), channel_id=3, replica_groups=mesh['dp_0'=2,'dp_1'=4,'dp_2'=2,'seq_0'=2,'seq_1'=8] {'seq_1'}, use_global_device_ids=true, to_apply=%add.1 | all-reduce | flops 16 | bytes 128
  194.6 0.1 reshape.88
  194.7 0.1 copy.39
  194.8 0.1 lt.30
  194.9 40.4 %reduce-scatter.4.cloned.1.call-done = f32[80,1280]{1,0:T(8,128)} async-done(((f32[1280,1280]{1,0:T(8,128)}), f32[80,1280]{1,0:T(8,128)}) %reduce-scatter.4.cloned.1.call-update) | async-done | bytes 409616 | tf_op jit(solution)/shard_map/reduce_scatter | solution.py:110
  235.3 1.7 convert_element_type.54
  237.1 0.3 copy.37
  237.3 0.2 copy.48
  237.6 0.1 fusion.28
  237.8 0.9 copy-done.8
  238.7 50.4 %while.11 = (s32[]{:T(128)}, bf16[8,512,1,80]{1,3,2,0:T(8,128)(2,1)S(1)}, bf16[8,512,1,80]{1,3,2,0:T(8,128)(2,1)S(1)}, bf16[4096,1,80]{0,2,1:T(8,128)(2,1)S(1)},...) while((s32[]{:T(128)}, bf16[8,512,1,80]{1,3,2,0:T(8,128)(2,1)S(1)}, ...), condition=%wide.region_5.6_spmd.clone, body=%wide.region_2.5_spmd.clone.sunk | while | flops 696298496 | bytes 26675348 | solution.py:74
  238.8 1.5 fusion.37
  240.3 2.2 fusion.38
  242.5 2.5 fusion.39
  245.0 0.1 iota_compare_fusion.3
  245.1 1.5 fusion.37
  246.6 2.2 fusion.38
  248.8 2.5 fusion.39
  251.4 1.5 fusion.37
  252.9 2.2 fusion.38
  255.1 2.5 fusion.39
  257.7 1.5 fusion.37
  259.2 2.2 fusion.38
  261.4 2.5 fusion.39
  264.0 1.5 fusion.37
  265.5 2.2 fusion.38
  267.7 2.5 fusion.39
  270.3 1.5 fusion.37
  271.8 2.2 fusion.38
  274.0 2.5 fusion.39
  276.6 1.5 fusion.37
  278.1 2.2 fusion.38
  280.3 2.5 fusion.39
  282.9 1.5 fusion.37
  284.4 2.2 fusion.38
  286.6 2.5 fusion.39
  289.1 0.4 copy.41
  289.5 0.2 all_to_all.31
  289.7 1.0 copy.42
  290.7 7.2 %all-to-all-start.1 = ((bf16[16,256,80]{1,2,0:T(8,128)(2,1)}), bf16[16,256,80]{1,2,0:T(8,128)(2,1)S(1)}, u32[]{:S(2)}, u32[]{:S(2)}) async-start(bf16[16,256,80]{1,2,0:T(8,128)(2,1)} %copy.42), calls=%async_computation.1 | async-start | bytes 1310720 | tf_op jit(solution)/shard_map/all_to_all | solution.py:99
  297.9 4.0 %copy.43 = bf16[2,4,2,80,1280]{4,3,2,1,0:T(8,128)(2,1)} copy(bf16[2,4,2,80,1280]{4,3,0,1,2:T(8,128)(2,1)} %bitcast.95) | data formatting | bytes 6553600 | tf_op jit(solution)/shard_map/transpose | solution.py:26
  301.9 40.0 %all-gather.17.cloned.1.call-done = bf16[1280,1280]{1,0:T(8,128)(2,1)} async-done(((bf16[80,1280]{1,0:T(8,128)(2,1)}), bf16[1280,1280]{1,0:T(8,128)(2,1)}) %all-gather.17.cloned.1.call-update) | async-done | bytes 3276816 | tf_op jit(solution)/shard_map/all_gather | solution.py:35
  341.9 3.2 convert_reduce_fusion
  345.1 3.9 %fusion.18 = bf16[1,256,1280]{2,1,0:T(8,128)(2,1)} fusion(bf16[256,1280]{0,1:T(8,128)(2,1)S(1)} %bitcast.102, bf16[1280,1280]{1,0:T(8,128)(2,1)} %bitcast.97, f32[256,640]{1,0:T(8,128)S(1)} %copy-done.5, f32[256,640]{1,0:T(8,128)S(1)} %copy-done.3, bf16[1,256,1280]{2,1,0:T(8,128)(2,1)S(1)} %copy-done.7), kind=kOutput, calls=%fused_computation.25 | convolution fusion | flops 840499200 | bytes 6553600 | tf_op jit(solution)/shard_map/dot_general | solution.py:101
  (57 shorter events, 1.0 us)
Async XLA Ops:
  7.2 12.4 %copy-start = (bf16[1,256,1280]{2,1,0:T(8,128)(2,1)S(1)}, bf16[1,256,1280]{2,1,0:T(8,128)(2,1)}, u32[]{:S(2)}) copy-start(bf16[1,256,1280]{2,1,0:T(8,128)(2,1)} %param.15) | copy-start | bytes 1966084
  7.2 88.6 %all-gather.11.cloned.1.call-start = ((), (), s32[]{:S(2)}) async-start(), calls=%async_computation.3 | async-start | bytes 10444800 | tf_op jit(solution)/shard_map/all_gather | solution.py:89
  7.9 117.3 %all-gather.13.cloned.1.call-start = ((), (), s32[]{:S(2)}) async-start(), calls=%async_computation.4 | async-start | bytes 2048000 | tf_op jit(solution)/shard_map/all_gather | solution.py:23
  18.9 216.5 %reduce-scatter.4.cloned.1.call-start = ((), (), s32[]{:S(2)}) async-start(), calls=%async_computation.7 | async-start | bytes 6963200 | tf_op jit(solution)/shard_map/reduce_scatter | solution.py:110
  32.9 0.7 copy-start.9
  32.9 3.1 copy-start.6
  35.9 59.9 %copy-start.4 = (f32[256,640]{1,0:T(8,128)}, f32[256,640]{1,0:T(8,128)S(1)}, u32[]{:S(2)}) copy-start(f32[256,640]{1,0:T(8,128)S(1)} %get-tuple-element.86) | copy-start | bytes 1966084
  35.9 67.7 %copy-start.2 = (f32[256,640]{1,0:T(8,128)}, f32[256,640]{1,0:T(8,128)S(1)}, u32[]{:S(2)}) copy-start(f32[256,640]{1,0:T(8,128)S(1)} %get-tuple-element.85) | copy-start | bytes 1966084
  117.6 8.6 %copy-start.11 = (u32[256]{0:T(256)S(1)}, u32[256]{0:T(256)}, u32[]{:S(2)}) copy-start(u32[256]{0:T(256)} %constant.42) | copy-start | bytes 3076
  117.6 14.5 %copy-start.10 = (u32[256]{0:T(256)S(1)}, u32[256]{0:T(256)}, u32[]{:S(2)}) copy-start(u32[256]{0:T(256)} %constant.47) | copy-start | bytes 3076
  117.6 119.5 %all-to-all-start = ((bf16[256,3,1280]{0,1,2:T(4,128)(2,1)}), bf16[256,3,1280]{0,1,2:T(4,128)(2,1)S(1)}, u32[]{:S(2)}, u32[]{:S(2)}) async-start(bf16[256,3,1280]{0,1,2:T(4,128)(2,1)} %copy.36), calls=%async_computation | async-start | bytes 5242880 | tf_op jit(solution)/shard_map/all_to_all | solution.py:95
  124.8 173.1 %all-gather.15.cloned.1.call-start = ((), (), s32[]{:S(2)}) async-start(), calls=%async_computation.5 | async-start | bytes 4915200 | tf_op jit(solution)/shard_map/all_gather | solution.py:23
  125.4 216.5 %all-gather.17.cloned.1.call-start = ((), (), s32[]{:S(2)}) async-start(), calls=%async_computation.6 | async-start | bytes 3481600 | tf_op jit(solution)/shard_map/all_gather | solution.py:35
  237.6 1.1 copy-start.8
  290.7 54.4 %all-to-all-start.1 = ((bf16[16,256,80]{1,2,0:T(8,128)(2,1)}), bf16[16,256,80]{1,2,0:T(8,128)(2,1)S(1)}, u32[]{:S(2)}, u32[]{:S(2)}) async-start(bf16[16,256,80]{1,2,0:T(8,128)(2,1)} %copy.42), calls=%async_computation.1 | async-start | bytes 1310720 | tf_op jit(solution)/shard_map/all_to_all | solution.py:99
  301.9 43.2 %copy-start.3 = (f32[256,640]{1,0:T(8,128)S(1)}, f32[256,640]{1,0:T(8,128)}, u32[]{:S(2)}) copy-start(f32[256,640]{1,0:T(8,128)} %copy-done.2) | copy-start | bytes 1966084
  301.9 43.2 %copy-start.5 = (f32[256,640]{1,0:T(8,128)S(1)}, f32[256,640]{1,0:T(8,128)}, u32[]{:S(2)}) copy-start(f32[256,640]{1,0:T(8,128)} %copy-done.4) | copy-start | bytes 1966084
  301.9 43.2 %copy-start.7 = (bf16[1,256,1280]{2,1,0:T(8,128)(2,1)S(1)}, bf16[1,256,1280]{2,1,0:T(8,128)(2,1)}, u32[]{:S(2)}) copy-start(bf16[1,256,1280]{2,1,0:T(8,128)(2,1)} %param.10) | copy-start | bytes 1966084
  345.1 3.9 %copy-start.1 = (bf16[1,256,1280]{2,1,0:T(8,128)(2,1)S(1)}, bf16[1,256,1280]{2,1,0:T(8,128)(2,1)}, u32[]{:S(2)}) copy-start(bf16[1,256,1280]{2,1,0:T(8,128)(2,1)} %param.15) | copy-start | bytes 1966084
Sparse Core Ops, SparseCore 0:
  10.7 85.0 all-gather.10
  97.6 27.6 all-gather.12
  129.7 105.5 reduce-scatter.3
  237.0 18.0 all-gather.14
  257.3 84.5 all-gather.16
where the time goes:
time: 356 us
  waiting for transfers between devices  141 us (40%)
  blocking collectives  76.5 us (21%)
  matrix products  48.9 us (14%)
  local copies, waits for them, and re-layouts  32.7 us (9%)
  other arithmetic  25.7 us (7%)
  between operations  15.9 us (4%)
  starting transfers between devices  14.6 us (4%)
    unnamed x2, blocking collectives  65.6 us
    all_gather x1, waiting for transfers between devices, on_device(): lax.all_gather(qkv_weight, DP, axis=0, tiled=True)  59.3 us
    reduce_scatter x1, waiting for transfers between devices, on_device(): lax.psum_scatter(lax.dot_general(column_part, masked_cot, (((0,), (0,)),...  40.4 us
    all_gather x1, waiting for transfers between devices, over_pieces(): return lax.all_gather(x, axis).astype(jnp.float32).sum(0)  40 us
    dot_general x8, matrix products, one_block(): jnp.einsum('hqk,khd->qhd', weights, value_rows, preferred_element_type=jn...  19.9 us
    reduce_sum x8, other arithmetic, one_block(): jnp.sum(exponent, axis=2, keepdims=True)  17.3 us
    dot_general x8, matrix products, one_block(): jnp.einsum('qhd,khd->hqk', block_query, key_rows, preferred_element_type=...  12.3 us
    unnamed x31, local copies, waits for them, and re-layouts  12.1 us
  transfers between devices with their start and end apart: 7, of which 4 were waited for; matrix products, arithmetic and copies ran while one was open for 29% of the time, Pallas kernels for 0%

commit v1 on v0

v1 whole, which is shorter than its diff:
```python
import functools
import math

import jax
import jax.numpy as jnp
from jax import lax
from jax.experimental import pallas as pl
from jax.experimental.pallas import tpu as pltpu
from jax.sharding import Mesh
from jax.sharding import PartitionSpec as P


HEADS = 16
YH, X, C, YL, Z = "dp_0", "dp_1", "dp_2", "seq_0", "seq_1"
DP = (YH, X, C)
SEQ = (YL, Z)
BF16 = jnp.bfloat16
F32 = jnp.float32


def shift(count, step):
    return [(i, (i + step) % count) for i in range(count)]


def swap_core(x):
    return lax.ppermute(x, C, [(0, 1), (1, 0)])


def swap_low(x):
    return lax.ppermute(x, YL, [(0, 1), (1, 0)])


def swap_cross(x):
    return lax.ppermute(x, (YH, YL), [(3, 0), (2, 1), (1, 2), (0, 3)])


def embed(tube_ids, model_width):
    half_width = model_width // 2
    positions = jnp.arange(half_width, dtype=F32)
    frequency = jnp.exp(positions * (-2.0 * math.log(10000.0) / model_width))
    angles = tube_ids.astype(F32)[:, None] * frequency[None, :]
    return jnp.concatenate([jnp.sin(angles), jnp.cos(angles)], axis=1)


def layer_norm(values):
    centered = values - jnp.mean(values, axis=1, keepdims=True)
    spread = jnp.mean(centered * centered, axis=1, keepdims=True)
    return centered * lax.rsqrt(spread + 1e-06)


def block_order(yh, x, c):
    ids = []
    for rc in range(2):
        for d in range(4):
            for ryh in range(2):
                ids.append((yh ^ ryh) * 8 + ((x - d) % 4) * 2 + (c ^ rc))
    return jnp.stack(ids).astype(jnp.int32)


def whole(*shape):
    return pl.BlockSpec(shape, lambda i, o: (0,) * len(shape))


def single(kernel, scalars, inputs, outputs, scratch):
    return pl.pallas_call(
        kernel,
        grid_spec=pltpu.PrefetchScalarGridSpec(
            num_scalar_prefetch=1,
            grid=(1,),
            in_specs=[whole(*x.shape) for x in inputs],
            out_specs=[whole(*o.shape) for o in outputs],
            scratch_shapes=scratch,
        ),
        out_shape=outputs,
    )(scalars, *inputs)


def turn_kernel(info, x_ref, o_ref, t_ref, p_ref):
    slots, width = x_ref.shape
    rows = width // HEADS
    t_ref[...] = x_ref[...].T
    for r in range(HEADS):
        start = pl.multiple_of(info[r] * rows, 16)
        p_ref[r * rows : (r + 1) * rows] = t_ref[pl.ds(start, rows), :]
    o_ref[:slots] = p_ref[...].T
    count = jnp.full((16, width), info[HEADS], jnp.int32)
    o_ref[slots:] = count.astype(F32).astype(BF16)


def turn_and_order(normed, order, count):
    slots, width = normed.shape
    out = jax.ShapeDtypeStruct((slots + 16, width), BF16)
    scratch = [pltpu.VMEM((width, slots), BF16), pltpu.VMEM((width, slots), BF16)]
    return single(turn_kernel, jnp.concatenate([order, count]), [normed], [out], scratch)[0]


def grad_kernel(order, factor, ab_ref, far_ref, own_ref, s1_ref, s2_ref, s3_ref, t_ref, m_ref):
    slots = ab_ref.shape[0] // 2
    rows = own_ref.shape[1]
    t_ref[:, :slots] = ab_ref[:slots, :].T
    t_ref[:, slots:] = far_ref[:slots, :].T
    m_ref[:slots, :] = ab_ref[slots:, :]
    m_ref[slots:, :] = far_ref[slots:, :]
    for r in range(8):
        start = pl.multiple_of(order[r] * rows, 16)
        part = jnp.dot(t_ref[pl.ds(start, rows), :], m_ref[...], preferred_element_type=F32) * factor
        if r < 2:
            own_ref[r] = part
        else:
            (s1_ref, s2_ref, s3_ref)[r // 2 - 1][r % 2] = part.astype(BF16)


def grad_pieces(order, factor, ab, far, rows):
    slots, width = ab.shape
    outs = [jax.ShapeDtypeStruct((2, rows, width), F32)] + [jax.ShapeDtypeStruct((2, rows, width), BF16)] * 3
    scratch = [pltpu.VMEM((width, slots), BF16), pltpu.VMEM((slots, width), BF16)]
    return single(lambda order, *refs: grad_kernel(order, factor, *refs), order, [ab, far], outs, scratch)


def project_kernel(_, ring_ref, far_ref, x_ref, y_ref, o_ref, *, kind, scale):
    half, outs = ring_ref.shape
    slots = x_ref.shape[0] - 16
    blocks = o_ref.shape[0]
    for k, v_ref in enumerate((x_ref, y_ref)):
        got = jnp.dot(v_ref[:slots, :half], ring_ref[...], preferred_element_type=F32)
        got = got + jnp.dot(v_ref[:slots, half:], far_ref[...], preferred_element_type=F32)
        if kind == "k":
            rows = outs // blocks
            lanes = slice(k * slots, (k + 1) * slots)
            o_ref[:, :rows, lanes] = got.astype(BF16).T.reshape(blocks, rows, slots)
            lane = lax.broadcasted_iota(jnp.int32, (16, slots), 1).astype(F32)
            row = lax.broadcasted_iota(jnp.int32, (16, slots), 0)
            bias = jnp.where((lane < v_ref[slots:, :slots].astype(F32)) | (row > 0), 0.0, -1e30).astype(BF16)
            o_ref[:, rows:, lanes] = jnp.broadcast_to(bias[None], (blocks, 16, slots))
        else:
            rows = outs // 2 // blocks
            lanes = slice(k * slots, (k + 1) * slots)
            o_ref[:, :rows, lanes] = got[:, : outs // 2].astype(BF16).T.reshape(blocks, rows, slots)
            query = (got[:, outs // 2 :] * scale).astype(BF16).T.reshape(blocks, rows, slots)
            part = slots // 2
            for h in range(2):
                at = (2 * h + k) * part
                o_ref[:, rows:, at : at + part] = query[:, :, h * part : (h + 1) * part]


def project(order, ring, far, near_x, far_x, z_count, kind, scale=None):
    pair = 2 * (near_x.shape[0] - 16)
    rows = ring.shape[1] // z_count + (16 if kind == "k" else 0)
    shapes = [jax.ShapeDtypeStruct((z_count, rows, pair), BF16)]
    kernel = functools.partial(project_kernel, kind=kind, scale=scale)
    return single(kernel, order, [ring, far, near_x, far_x], shapes, [])[0]


def attend_kernel(info, q_ref, k_ref, v_ref, *rest, key_block):
    blocks, tall, pair = k_ref.shape
    t_ref = rest[0] if len(rest) > 4 else None
    o_ref, kt_ref, ka_ref, va_ref = rest[-4:]
    group, head_width, part = q_ref.shape
    lanes = ka_ref.shape[1]
    extra = va_ref.shape[0] - head_width
    tile = group * part
    yl = info[0]

    @pl.when(pl.program_id(0) == 0)
    def _():
        kt_ref[...] = jnp.zeros_like(kt_ref)
        row = lax.broadcasted_iota(jnp.int32, (extra, pair), 0)
        for s in range(blocks):
            kt_ref[:tall, :] = k_ref[s]
            ka_ref[pl.ds(s * pair, pair), :] = kt_ref[...].T
            va_ref[:head_width, pl.ds(s * pair, pair)] = v_ref[s]
            va_ref[head_width:, pl.ds(s * pair, pair)] = jnp.where(row == 0, 1.0, 0.0).astype(BF16)

    ones = jnp.where(lax.broadcasted_iota(jnp.int32, (lanes - head_width, tile), 0) == 0, 1.0, 0.0)
    query = jnp.concatenate([q_ref[g] for g in range(group)], axis=1)
    query = jnp.concatenate([query, ones.astype(BF16)], axis=0)
    keys = ka_ref.shape[0]
    steps = keys // key_block

    def scores_of(j):
        return jnp.dot(ka_ref[pl.ds(j * key_block, key_block), :], query, preferred_element_type=F32)

    top = jnp.full((1, tile), -1e30, F32)
    total = jnp.zeros((head_width + extra, tile), F32)
    ahead = scores_of(0)
    for j in range(steps):
        scores = ahead
        if j + 1 < steps:
            ahead = scores_of(j + 1)
        new_top = jnp.maximum(top, jnp.max(scores, axis=0, keepdims=True))
        weights = jnp.exp2(scores - new_top).astype(BF16)
        got = jnp.dot(va_ref[:, pl.ds(j * key_block, key_block)], weights, preferred_element_type=F32)
        total = total * jnp.exp2(top - new_top) + got
        top = new_top
    context = (total[:head_width] / total[head_width : head_width + 1]).astype(BF16)
    half = part // 2
    for g in range(group):
        o_ref[yl, g, :head_width] = context[:, g * part : g * part + half]
        o_ref[1 - yl, g, :head_width] = context[:, g * part + half : (g + 1) * part]
    if t_ref is not None:
        o_ref[:, :, head_width:] = t_ref[...]


def attend(info, h, k, vq, tiles=None):
    blocks, _, pair = k.shape
    head_width = vq.shape[1] // 2
    part = pair // 2
    group = 4
    keys = blocks * pair
    in_specs = [
        pl.BlockSpec((group, head_width, part), lambda i, o: (i, 1, h)),
        whole(*k.shape),
        pl.BlockSpec((blocks, head_width, pair), lambda i, o: (0, 0, 0)),
    ]
    args = [vq, k, vq]
    rows = head_width
    if tiles is not None:
        extra = tiles.shape[2]
        in_specs.append(pl.BlockSpec((2, group, extra, 128), lambda i, o: (0, i, 0, 0)))
        args.append(tiles)
        rows += extra
    return pl.pallas_call(
        functools.partial(attend_kernel, key_block=512),
        grid_spec=pltpu.PrefetchScalarGridSpec(
            num_scalar_prefetch=1,
            grid=(blocks // group,),
            in_specs=in_specs,
            out_specs=pl.BlockSpec((2, group, rows, part // 2), lambda i, o: (0, i, 0, 0)),
            scratch_shapes=[
                pltpu.VMEM((128, pair), BF16),
                pltpu.VMEM((keys, 128), BF16),
                pltpu.VMEM((head_width + 16, keys), BF16),
            ],
        ),
        out_shape=jax.ShapeDtypeStruct((2, blocks, rows, part // 2), BF16),
        compiler_params=pltpu.CompilerParams(dimension_semantics=("arbitrary",)),
        name="attend",
    )(info, *args)


def tile_kernel(_, own_ref, got_ref, o_ref):
    rows, width = own_ref.shape
    total = (own_ref[...] + got_ref[...].astype(F32)).astype(BF16)
    across = width // 128
    per = o_ref.shape[2] // 16
    count = (rows // 16) * across
    for t in range(2 * o_ref.shape[1] * per):
        group, at = divmod(t, per)
        if t < count:
            r, l = divmod(t, across)
            piece = total[16 * r : 16 * r + 16, 128 * l : 128 * l + 128]
        else:
            piece = jnp.zeros((16, 128), BF16)
        o_ref[group // o_ref.shape[1], group % o_ref.shape[1], 16 * at : 16 * at + 16] = piece


def finish_kernel(order, c_ref, ring_ref, far_ref, w_ref, *refs):
    o_ref = refs[0]
    t_ref = refs[-1]
    half = ring_ref.shape[0]
    rows = half // 8
    for r in range(HEADS):
        t_ref[r * rows : (r + 1) * rows] = c_ref[order[r], :rows]
    context = t_ref[...].T
    mixed = jnp.dot(context[:, :half], ring_ref[...], preferred_element_type=F32)
    mixed = mixed + jnp.dot(context[:, half:], far_ref[...], preferred_element_type=F32)
    o_ref[...] = (w_ref[...] + mixed).astype(BF16)
    if len(refs) == 3:
        g_ref = refs[1]
        across = g_ref.shape[1] // 128
        per = (c_ref.shape[1] - rows) // 16
        for t in range((g_ref.shape[0] // 16) * across):
            group, at = divmod(t, per)
            r, l = divmod(t, across)
            piece = c_ref[group, rows + 16 * at : rows + 16 * at + 16]
            g_ref[16 * r : 16 * r + 16, 128 * l : 128 * l + 128] = piece.astype(F32)


def after(value, *others):
    return lax.optimization_barrier((value, *others))[0]


def x_ring(pieces):
    return [lax.ppermute(p, X, shift(4, d)) for d, p in zip((1, 2, 3), pieces)]


def on_device(tokens, tube_index, counts, qkv_weight, proj_weight, ctx_b, cot_b, b_counts):
    slots = tokens.shape[1]
    width = tokens.shape[2]
    z_count = lax.axis_size(Z)
    rows = qkv_weight.shape[0]
    head_width = width // HEADS
    half_width = width // 2
    yh, x, c, yl = (lax.axis_index(a) for a in (YH, X, C, YL))
    order = block_order(yh, x, c)

    def columns(part, side):
        return lax.dynamic_slice(qkv_weight, (0, part * width + side * half_width), (rows, half_width))

    near_k = columns(1, yl)
    cross_k = swap_cross(columns(1, 1 - yl))

    with_pos = tokens[0].astype(F32) + embed(tube_index[0], width)
    normed = layer_norm(with_pos).astype(BF16)
    turned = turn_and_order(normed, order, counts[0])
    other = swap_low(turned)

    def ring_of(pair, got):
        return jnp.stack([pair] + got).reshape(-1, pair.shape[2])

    pair_k = jnp.stack([near_k, cross_k])
    got_k = x_ring([pair_k] * 3)
    ring_k = ring_of(pair_k, got_k)
    far_k = swap_core(ring_k)

    rest = jnp.concatenate([columns(2, 1 - yl), columns(0, 1 - yl), proj_weight], axis=1)
    cross_rest = swap_cross(after(rest, pair_k))

    row_ids = lax.broadcasted_iota(jnp.int32, (slots, 1), 0)
    local_cot = after(cot_b[0], turned)
    masked_cot = jnp.where(row_ids < b_counts[0, 0], local_cot, jnp.zeros((), BF16))
    both_b = jnp.concatenate([ctx_b[0], masked_cot])
    far_b = swap_core(both_b)

    made_k = project(order, ring_k, far_k, turned, other, z_count, "k")
    keys = lax.all_to_all(made_k, Z, 0, 0, tiled=True)

    near_vq = jnp.concatenate([columns(2, yl), columns(0, yl)], axis=1)
    pair_vq = after(jnp.stack([near_vq, cross_rest[:, :width]]), *got_k)
    got_vq = x_ring([pair_vq] * 3)
    got_vq = list(lax.optimization_barrier((*got_vq, made_k))[:3])
    ring_vq = ring_of(pair_vq, got_vq)
    far_vq = swap_core(ring_vq)

    factor = 1.0 / math.sqrt(lax.axis_size(DP) * lax.axis_size(SEQ) * slots)
    targets = []
    for d in range(4):
        for ryh in range(2):
            targets.append((yh ^ ryh) * 8 + ((x + d) % 4) * 2 + c)
    own, *sends = grad_pieces(jnp.stack(targets).astype(jnp.int32), factor, both_b, after(far_b, made_k), rows)

    q_scale = math.log2(math.e) / math.sqrt(head_width)
    made_vq = project(order, ring_vq, after(far_vq, own), turned, other, z_count, "vq", q_scale)
    values = lax.all_to_all(made_vq, Z, 0, 0, tiled=True)

    got_g = x_ring(lax.optimization_barrier((*sends, *got_vq))[:3])
    for g in got_g:
        own = own + g.astype(F32)
    pair_p = after(jnp.stack([proj_weight, cross_rest[:, width:]]), *got_g)
    got_p = x_ring([pair_p] * 3)
    tiles = single(
        tile_kernel,
        order,
        [own[0], after(swap_cross(own[1]), pair_p)],
        [jax.ShapeDtypeStruct((2, z_count, 64, 128), BF16)],
        [],
    )[0]
    ring_p = ring_of(pair_p, got_p)
    far_p = swap_core(ring_p)

    half = slots // 2

    def finish(context, h, done=None):
        kernel = finish_kernel
        args = [context, ring_p, far_p, with_pos]
        specs = [
            whole(*context.shape),
            whole(*ring_p.shape),
            whole(*far_p.shape),
            pl.BlockSpec((half, width), lambda i, o: (h, 0)),
        ]
        outs = [jax.ShapeDtypeStruct((slots, width), BF16)]
        out_specs = [pl.BlockSpec((half, width), lambda i, o: (h, 0))]
        aliases = {}
        if done is not None:
            kernel = lambda order, c, r, f, w, d, *refs: finish_kernel(order, c, r, f, w, *refs)
            args.append(done)
            specs.append(pl.BlockSpec(memory_space=pl.ANY))
            outs.append(jax.ShapeDtypeStruct((rows, width), F32))
            out_specs.append(whole(rows, width))
            aliases = {5: 0}
        return pl.pallas_call(
            kernel,
            grid_spec=pltpu.PrefetchScalarGridSpec(
                num_scalar_prefetch=1,
                grid=(1,),
                in_specs=specs,
                out_specs=out_specs,
                scratch_shapes=[pltpu.VMEM((width, half), BF16)],
            ),
            out_shape=outs,
            input_output_aliases=aliases,
            name="finish",
        )(order, *args)

    info = yl.reshape(1).astype(jnp.int32)
    first = attend(info, 0, keys, values, tiles).reshape(HEADS, -1, half)
    first = lax.all_to_all(first, SEQ, 0, 0, tiled=True)
    second = attend(info, 1, keys, values).reshape(HEADS, -1, half)
    summed = first[:, head_width:].astype(F32).sum(0).astype(BF16)
    second = jnp.concatenate([second, jnp.broadcast_to(summed[None], (HEADS, 64, 128))], axis=1)
    second = lax.all_to_all(second, SEQ, 0, 0, tiled=True)
    out_first = finish(first, 0)[0]
    out_a, weight_grad = finish(second, 1, out_first)
    return (out_a[None], weight_grad)


def solution(mesh):
    split = Mesh(mesh.devices.reshape(2, 4, 2, 2, 8), ("dp_0", "dp_1", "dp_2", "seq_0", "seq_1"))
    return jax.shard_map(
        on_device,
        mesh=split,
        in_specs=(
            P(DP, SEQ, None),
            P(DP, SEQ),
            P(DP, SEQ),
            P(DP, None),
            P(DP, None),
            P(DP, SEQ, None),
            P(DP, SEQ, None),
            P(DP, SEQ),
        ),
        out_specs=(P(DP, SEQ, None), P(DP, None)),
        check_vma=False,
    )
```

time: 356 us -> 221 us (0.62)
  blocking collectives: 76.5 us -> 0 us
  waiting for transfers between devices: 141 us -> 81.1 us
  Pallas kernels: 0 us -> 55.9 us
  matrix products: 48.9 us -> 0 us
  starting transfers between devices: 14.6 us -> 55.5 us
  local copies, waits for them, and re-layouts: 32.7 us -> 11.4 us
  other arithmetic: 25.7 us -> 11.8 us
  between operations: 15.9 us -> 2.23 us
    all_gather x4 -> x0, waiting for transfers between devices: 99.6 us -> none  [the longest x1 59.3 us: on_device(): lax.all_gather(qkv_weight, DP, axis=0, tiled=True)]
    unnamed x2 -> x0, blocking collectives: 65.6 us -> none
    ppermute x0 -> x20, waiting for transfers between devices: none -> 63.6 us  [the longest x12 52 us: x_ring(): return [lax.ppermute(p, X, shift(4, d)) for d, p in zip((1, 2, 3), pieces)]]
    pallas_call x0 -> x9, Pallas kernels: none -> 55.9 us  [the longest x2 24.9 us: attend(): pl.pallas_call(functools.partial(attend_kernel, key_block=512), grid_spec...]
    dot_general x19 -> x0, matrix products: 48.9 us -> none  [the longest x8 19.9 us: one_block(): jnp.einsum('hqk,khd->qhd', weights, value_rows, preferred_element_type=jn...]
    reduce_scatter x1 -> x0, waiting for transfers between devices: 40.4 us -> none  [on_device(): lax.psum_scatter(lax.dot_general(column_part, masked_cot, (((0,), (0,)),...]
    ppermute x0 -> x20, starting transfers between devices: none -> 28.4 us  [the longest x12 20.4 us: x_ring(): return [lax.ppermute(p, X, shift(4, d)) for d, p in zip((1, 2, 3), pieces)]]
    reduce_sum x9 -> x1, other arithmetic: 20.5 us -> 1 us  [on_device(): summed = first[:, head_width:].astype(F32).sum(0).astype(BF16)]
  transfers between devices with their start and end apart: 7 -> 24, of which waited for: 4 -> 15; matrix products, arithmetic and copies ran while one was open for 29% -> 6% of each run, Pallas kernels for 0% -> 18%
where the time goes in v1:
time: 221 us; the launch traced here: 218 us
  waiting for transfers between devices  81.1 us (37%)
  Pallas kernels  55.9 us (25%)
  starting transfers between devices  55.5 us (25%)
  other arithmetic  11.8 us (5%)
  local copies, waits for them, and re-layouts  11.4 us (5%)
  between operations  2.23 us (1%)
    ppermute x12, waiting for transfers between devices, x_ring(): return [lax.ppermute(p, X, shift(4, d)) for d, p in zip((1, 2, 3), pieces)]  52 us
    pallas_call x2, Pallas kernels, attend(): pl.pallas_call(functools.partial(attend_kernel, key_block=512), grid_spec...  24.9 us
    pallas_call x5, Pallas kernels, single(): pl.pallas_call(kernel, grid_spec=pltpu.PrefetchScalarGridSpec(num_scalar_...  22.2 us
    ppermute x12, starting transfers between devices, x_ring(): return [lax.ppermute(p, X, shift(4, d)) for d, p in zip((1, 2, 3), pieces)]  20.4 us
    all_to_all x1, waiting for transfers between devices, on_device(): second = lax.all_to_all(second, SEQ, 0, 0, tiled=True)  11.7 us
    ppermute x3, waiting for transfers between devices, swap_cross(): return lax.ppermute(x, (YH, YL), [(3, 0), (2, 1), (1, 2), (0, 3)])  8.85 us
    pallas_call x2, Pallas kernels, finish(): pl.pallas_call(kernel, grid_spec=pltpu.PrefetchScalarGridSpec(num_scalar_...  8.85 us
    all_to_all x1, starting transfers between devices, on_device(): keys = lax.all_to_all(made_k, Z, 0, 0, tiled=True)  8.47 us
  transfers between devices with their start and end apart: 24, of which 15 were waited for; matrix products, arithmetic and copies ran while one was open for 6% of the time, Pallas kernels for 18%

profile of v1, /device:TPU:4, one launch (start us, length us, event | category | flops | bytes accessed | tf_op | source)
XLA Modules:
  0.0 217.8 jit_solution(2648498132852054378)
XLA Ops:
  0.7 1.3 constant_dynamic-slice_fusion.4
  1.9 3.1 %collective-permute-start = (bf16[80,640]{1,0:T(8,128)(2,1)S(1)}, bf16[80,640]{1,0:T(8,128)(2,1)S(1)}, u32[]{:S(2)}, u32[]{:S(2)}) collective-permute-start(bf16[80,640]{1,0:T(8,128)(2,1)S(1)} %get-tuple-element.48), channel_id=1, source_target_pairs={{136,0},{128,8},{8,128},{0,136},{137,1},{129,9},{9,129},{1,137},{1... | collective-permute-start | bytes 307208 | tf_op jit(solution)/shard_map/ppermute | solution.py:34
  5.0 0.7 convert_element_type.32
  5.7 2.3 %multiply_sine_fusion = (f32[256,640]{1,0:T(8,128)S(1)}, f32[256,640]{1,0:T(8,128)S(1)}) fusion(f32[640]{0:T(1024)S(1)} %multiply_exponential_fusion, f32[256]{0:T(256)S(1)} %bitcast.91), kind=kLoop, calls=%fused_computation.7 | loop fusion | flops 163840 | bytes 1314304 | tf_op jit(solution)/shard_map/sin | solution.py:42
  8.6 0.8 copy-done.9
  9.6 1.4 collective-permute-start.1
  11.0 1.0 multiply_convert_fusion.x_ref
  12.7 0.7 concatenate.21.info
  13.4 3.0 %shard_map.95.x_ref = bf16[272,1280]{1,0:T(8,128)(2,1)} custom-call(s32[17]{0:T(128)} %concatenate.21.info, bf16[256,1280]{1,0:T(8,128)(2,1)} %multiply_convert_fusion.x_ref), custom_call_target="tpu_custom_call" | custom-call | tf_op jit(solution)/shard_map/pallas_call | solution.py:65
  16.5 0.5 collective-permute-start.4
  17.0 2.7 %collective-permute-start.3 = (bf16[2,80,640]{2,1,0:T(8,128)(2,1)S(1)}, bf16[2,80,640]{2,1,0:T(8,128)(2,1)S(1)}, u32[]{:S(2)}, u32[]{:S(2)}) collective-permute-start(bf16[2,80,640]{2,1,0:T(8,128)(2,1)S(1)} %get-tuple-element.53), channel_id=1, source_target_pairs={{0,64},{32,96},{64,0},{96,32},{1,65},{33,97},{65,1},{97,33},{2,66}... | collective-permute-start | bytes 614408 | tf_op jit(solution)/shard_map/ppermute | solution.py:284
  19.7 0.4 collective-permute-start.2
  20.2 3.9 %collective-permute-done.4 = bf16[2,80,640]{2,1,0:T(8,128)(2,1)S(1)} collective-permute-done((bf16[2,80,640]{2,1,0:T(8,128)(2,1)S(1)}, bf16[2,80,640]{2,1,0:T(8,128)(2,1)S(1)}, u32[]{:S(2)}, u32[]{:S(2)}) %collective-permute-start.4) | collective-permute-done | bytes 204832 | tf_op jit(solution)/shard_map/ppermute | solution.py:284
  24.0 1.9 collective-permute-done.3
  25.9 2.1 collective-permute-done.2
  28.2 0.9 slice_bitcast_fusion.2
  29.1 0.6 collective-permute-start.7
  29.8 2.8 %collective-permute-start.6 = (bf16[2,80,1280]{2,1,0:T(8,128)(2,1)S(1)}, bf16[2,80,1280]{2,1,0:T(8,128)(2,1)S(1)}, u32[]{:S(2)}, u32[]{:S(2)}) collective-permute-start(bf16[2,80,1280]{2,1,0:T(8,128)(2,1)S(1)} %pad_maximum_fusion.6), channel_id=1, source_target_pairs={{0,64},{32,96},{64,0},{96,32},{1,65},{33,97},{65,1},{97,33},{2,66}... | collective-permute-start | bytes 1228808 | tf_op jit(solution)/shard_map/ppermute | solution.py:284
  32.6 2.0 collective-permute-start.5
  34.6 0.7 stack.162._.order
  36.0 0.8 copy-done.7
  36.8 4.8 %shard_map.96 = bf16[8,96,512]{2,1,0:T(8,128)(2,1)} custom-call(s32[16]{0:T(128)} %stack.162._.order, bf16[640,640]{1,0:T(8,128)(2,1)} %bitcast.73, bf16[640,640]{1,0:T(8,128)(2,1)} %collective-permute-done.8.far_ref, bf16[272,1280]{1,0:T(8,128)(2,1)} %shard_map.95.x_ref, bf16[272,1280]{1,0:T(8,128)(2,1)} %copy-done.7), custom_call_target="tpu_custom_call" | custom-call | tf_op jit(solution)/shard_map/pallas_call | solution.py:65
  41.6 2.0 collective-permute-done.6
  43.7 7.9 %collective-permute-done.5 = bf16[2,80,1280]{2,1,0:T(8,128)(2,1)} collective-permute-done((bf16[2,80,1280]{2,1,0:T(8,128)(2,1)S(1)}, bf16[2,80,1280]{2,1,0:T(8,128)(2,1)}, u32[]{:S(2)}, u32[]{:S(2)}) %collective-permute-start.5) | collective-permute-done | bytes 409632 | tf_op jit(solution)/shard_map/ppermute | solution.py:284
  51.6 1.3 pad_maximum_fusion
  52.9 0.3 collective-permute-start.10
  53.3 0.8 copy-done.4
  54.1 8.5 %all-to-all-start.1 = ((bf16[8,96,512]{2,1,0:T(8,128)(2,1)}), bf16[8,96,512]{2,1,0:T(8,128)(2,1)S(1)}, u32[]{:S(2)}, u32[]{:S(2)}) async-start(bf16[8,96,512]{2,1,0:T(8,128)(2,1)} %shard_map.96), calls=%async_computation.1 | async-start | bytes 1572864 | tf_op jit(solution)/shard_map/all_to_all | solution.py:326
  62.5 2.3 %pad_maximum_fusion.2.refs_0_ = bf16[512,1280]{1,0:T(8,128)(2,1)} fusion(bf16[256,1280]{1,0:T(8,128)(2,1)S(1)} %broadcast_select_fusion, bf16[256,1280]{1,0:T(8,128)(2,1)} %bitcast.80), kind=kLoop, calls=%fused_computation.3 | loop fusion | flops 2621440 | bytes 2621440 | tf_op jit(solution)/shard_map/concatenate | solution.py:322
  64.8 0.6 stack.185.order
  65.4 2.7 %collective-permute-done.11.refs_1_ = bf16[512,1280]{1,0:T(8,128)(2,1)} collective-permute-done((bf16[512,1280]{1,0:T(8,128)(2,1)}, bf16[512,1280]{1,0:T(8,128)(2,1)}, u32[]{:S(2)}, u32[]{:S(2)}) %collective-permute-start.11) | collective-permute-done | bytes 1310752 | tf_op jit(solution)/shard_map/ppermute | solution.py:26
  68.2 5.4 %shard_map.97 = (f32[2,80,1280]{2,1,0:T(8,128)}, bf16[2,80,1280]{2,1,0:T(8,128)(2,1)}, bf16[2,80,1280]{2,1,0:T(8,128)(2,1)}, bf16[2,80,1280]{2,1,0:T(8,128)(2,1)}) custom-call(s32[8]{0:T(128)} %stack.185.order, bf16[512,1280]{1,0:T(8,128)(2,1)} %pad_maximum_fusion.2.refs_0_, bf16[512,1280]{1,0:T(8,128)(2,1)} %collective-permute-done.11.refs_1_), custom_call_target="tpu_custom_call" | custom-call | tf_op jit(solution)/shard_map/pallas_call | solution.py:65
  73.6 6.3 %shard_map.98 = bf16[8,160,512]{2,1,0:T(8,128)(2,1)} custom-call(s32[16]{0:T(128)} %stack.162._.order, bf16[640,1280]{1,0:T(8,128)(2,1)} %bitcast.71, bf16[640,1280]{1,0:T(8,128)(2,1)} %collective-permute-done.10.far_ref, bf16[272,1280]{1,0:T(8,128)(2,1)} %shard_map.95.x_ref, bf16[272,1280]{1,0:T(8,128)(2,1)} %copy-done.7), custom_call_target="tpu_custom_call" | custom-call | tf_op jit(solution)/shard_map/pallas_call | solution.py:65
  80.0 5.9 %all-to-all-done.1.k_ref = bf16[8,96,512]{2,1,0:T(8,128)(2,1)S(1)} async-done(((bf16[8,96,512]{2,1,0:T(8,128)(2,1)}), bf16[8,96,512]{2,1,0:T(8,128)(2,1)S(1)}, u32[]{:S(2)}, u32[]{:S(2)}) %all-to-all-start.1) | async-done | bytes 786464 | tf_op jit(solution)/shard_map/all_to_all | solution.py:326
  85.8 0.9 copy-done.3
  86.7 3.6 %all-to-all-start = ((bf16[8,160,512]{2,1,0:T(8,128)(2,1)}), bf16[8,160,512]{2,1,0:T(8,128)(2,1)S(1)}, u32[]{:S(2)}, u32[]{:S(2)}) async-start(bf16[8,160,512]{2,1,0:T(8,128)(2,1)} %shard_map.98), calls=%async_computation | async-start | bytes 2621440 | tf_op jit(solution)/shard_map/all_to_all | solution.py:344
  90.3 1.3 collective-permute-start.12
  91.6 1.7 collective-permute-start.13
  93.3 2.5 %collective-permute-start.14 = (bf16[2,80,1280]{2,1,0:T(8,128)(2,1)}, bf16[2,80,1280]{2,1,0:T(8,128)(2,1)S(1)}, u32[]{:S(2)}, u32[]{:S(2)}) collective-permute-start(bf16[2,80,1280]{2,1,0:T(8,128)(2,1)} %get-tuple-element.35), channel_id=1, source_target_pairs={{0,96},{32,0},{64,32},{96,64},{1,97},{33,1},{65,33},{97,65},{2,98}... | collective-permute-start | bytes 1228808 | tf_op jit(solution)/shard_map/ppermute | solution.py:284
  95.8 6.2 %collective-permute-done.12 = bf16[2,80,1280]{2,1,0:T(8,128)(2,1)S(1)} collective-permute-done((bf16[2,80,1280]{2,1,0:T(8,128)(2,1)}, bf16[2,80,1280]{2,1,0:T(8,128)(2,1)S(1)}, u32[]{:S(2)}, u32[]{:S(2)}) %collective-permute-start.12) | collective-permute-done | bytes 409632 | tf_op jit(solution)/shard_map/ppermute | solution.py:284
  102.0 9.8 %collective-permute-done.13 = bf16[2,80,1280]{2,1,0:T(8,128)(2,1)S(1)} collective-permute-done((bf16[2,80,1280]{2,1,0:T(8,128)(2,1)}, bf16[2,80,1280]{2,1,0:T(8,128)(2,1)S(1)}, u32[]{:S(2)}, u32[]{:S(2)}) %collective-permute-start.13) | collective-permute-done | bytes 409632 | tf_op jit(solution)/shard_map/ppermute | solution.py:284
  111.8 0.9 collective-permute-done.14
  112.9 0.8 slice_bitcast_fusion
  113.7 2.7 %collective-permute-start.15 = (f32[80,1280]{1,0:T(8,128)S(1)}, f32[80,1280]{1,0:T(8,128)S(1)}, u32[]{:S(2)}, u32[]{:S(2)}) collective-permute-start(f32[80,1280]{1,0:T(8,128)S(1)} %get-tuple-element.42), channel_id=1, source_target_pairs={{136,0},{128,8},{8,128},{0,136},{137,1},{129,9},{9,129},{1,137},{1... | collective-permute-start | bytes 1228808 | tf_op jit(solution)/shard_map/ppermute | solution.py:34
  116.5 8.8 %collective-permute-done.15.got_ref = f32[80,1280]{1,0:T(8,128)S(1)} collective-permute-done((f32[80,1280]{1,0:T(8,128)S(1)}, f32[80,1280]{1,0:T(8,128)S(1)}, u32[]{:S(2)}, u32[]{:S(2)}) %collective-permute-start.15) | collective-permute-done | bytes 409632 | tf_op jit(solution)/shard_map/ppermute | solution.py:34
  125.4 0.7 copy-done.13
  126.1 2.5 %shard_map.99.rest_0_ = bf16[2,8,64,128]{3,2,1,0:T(8,128)(2,1)} custom-call(s32[16]{0:T(128)} %stack.162._.order, f32[80,1280]{1,0:T(8,128)} %get-tuple-element.43.own_ref, f32[80,1280]{1,0:T(8,128)} %copy-done.13), custom_call_target="tpu_custom_call" | custom-call | tf_op jit(solution)/shard_map/pallas_call | solution.py:65
  128.7 1.1 copy-done
  129.7 12.4 %attend.3 = bf16[2,8,144,128]{3,2,1,0:T(8,128)(2,1)} custom-call(s32[1]{0:T(128)} %bitcast.16.info, bf16[8,160,512]{2,1,0:T(8,128)(2,1)} %copy-done, bf16[8,96,512]{2,1,0:T(8,128)(2,1)} %copy-done.3, bf16[8,160,512]{2,1,0:T(8,128)(2,1)} %copy-done, bf16[2,8,64,128]{3,2,1,0:T(8,128)(2,1)} %shard_map.99.rest_0_), custom_call_target="tpu_custom_call" | custom-call | tf_op jit(solution)/shard_map/attend/pallas_call | solution.py:222
  142.1 7.3 %all-to-all-start.2 = ((bf16[16,144,128]{2,1,0:T(8,128)(2,1)}), bf16[16,144,128]{2,1,0:T(8,128)(2,1)}, u32[]{:S(2)}, u32[]{:S(2)}) async-start(bf16[16,144,128]{2,1,0:T(8,128)(2,1)} %bitcast.75), calls=%async_computation.2 | async-start | bytes 1179648 | tf_op jit(solution)/shard_map/all_to_all | solution.py:398
  149.4 2.4 %collective-permute-start.18 = (bf16[2,80,1280]{2,1,0:T(8,128)(2,1)S(1)}, bf16[2,80,1280]{2,1,0:T(8,128)(2,1)S(1)}, u32[]{:S(2)}, u32[]{:S(2)}) collective-permute-start(bf16[2,80,1280]{2,1,0:T(8,128)(2,1)S(1)} %pad_maximum_fusion.7), channel_id=1, source_target_pairs={{0,96},{32,0},{64,32},{96,64},{1,97},{33,1},{65,33},{97,65},{2,98}... | collective-permute-start | bytes 1228808 | tf_op jit(solution)/shard_map/ppermute | solution.py:284
  151.9 3.3 %collective-permute-start.17 = (bf16[2,80,1280]{2,1,0:T(8,128)(2,1)S(1)}, bf16[2,80,1280]{2,1,0:T(8,128)(2,1)S(1)}, u32[]{:S(2)}, u32[]{:S(2)}) collective-permute-start(bf16[2,80,1280]{2,1,0:T(8,128)(2,1)S(1)} %pad_maximum_fusion.7), channel_id=1, source_target_pairs={{0,64},{32,96},{64,0},{96,32},{1,65},{33,97},{65,1},{97,33},{2,66}... | collective-permute-start | bytes 1228808 | tf_op jit(solution)/shard_map/ppermute | solution.py:284
  155.1 8.2 %collective-permute-done.18 = bf16[2,80,1280]{2,1,0:T(8,128)(2,1)S(1)} collective-permute-done((bf16[2,80,1280]{2,1,0:T(8,128)(2,1)S(1)}, bf16[2,80,1280]{2,1,0:T(8,128)(2,1)S(1)}, u32[]{:S(2)}, u32[]{:S(2)}) %collective-permute-start.18) | collective-permute-done | bytes 409632 | tf_op jit(solution)/shard_map/ppermute | solution.py:284
  163.4 2.4 %collective-permute-done.17 = bf16[2,80,1280]{2,1,0:T(8,128)(2,1)S(1)} collective-permute-done((bf16[2,80,1280]{2,1,0:T(8,128)(2,1)S(1)}, bf16[2,80,1280]{2,1,0:T(8,128)(2,1)S(1)}, u32[]{:S(2)}, u32[]{:S(2)}) %collective-permute-start.17) | collective-permute-done | bytes 409632 | tf_op jit(solution)/shard_map/ppermute | solution.py:284
  165.7 6.6 %collective-permute-done.16 = bf16[2,80,1280]{2,1,0:T(8,128)(2,1)S(1)} collective-permute-done((bf16[2,80,1280]{2,1,0:T(8,128)(2,1)S(1)}, bf16[2,80,1280]{2,1,0:T(8,128)(2,1)S(1)}, u32[]{:S(2)}, u32[]{:S(2)}) %collective-permute-start.16) | collective-permute-done | bytes 409632 | tf_op jit(solution)/shard_map/ppermute | solution.py:284
  172.6 0.4 collective-permute-start.19
  173.0 12.5 %attend.2 = bf16[2,8,80,128]{3,2,1,0:T(8,128)(2,1)} custom-call(s32[1]{0:T(128)} %bitcast.16.info, bf16[8,160,512]{2,1,0:T(8,128)(2,1)} %copy-done, bf16[8,96,512]{2,1,0:T(8,128)(2,1)} %copy-done.3, bf16[8,160,512]{2,1,0:T(8,128)(2,1)} %copy-done), custom_call_target="tpu_custom_call" | custom-call | tf_op jit(solution)/shard_map/attend/pallas_call | solution.py:222
  185.4 1.0 slice_reduce_fusion
  186.5 1.8 pad_maximum_fusion.4
  188.3 7.8 %all-to-all-start.3 = ((bf16[16,144,128]{2,1,0:T(8,128)(2,1)}), bf16[16,144,128]{2,1,0:T(8,128)(2,1)}, u32[]{:S(2)}, u32[]{:S(2)}) async-start(bf16[16,144,128]{2,1,0:T(8,128)(2,1)} %pad_maximum_fusion.4), calls=%async_computation.3 | async-start | bytes 1179648 | tf_op jit(solution)/shard_map/all_to_all | solution.py:402
  196.1 1.2 copy-done.5
  197.3 4.4 %finish.2.d = bf16[256,1280]{1,0:T(8,128)(2,1)} custom-call(s32[16]{0:T(128)} %stack.162._.order, bf16[16,144,128]{2,1,0:T(8,128)(2,1)} %all-to-all-done.2.c_ref, bf16[640,1280]{1,0:T(8,128)(2,1)} %bitcast.68, bf16[640,1280]{1,0:T(8,128)(2,1)} %copy-done.5, f32[256,1280]{1,0:T(8,128)} %copy-done.1), custom_call_target="tpu_custom_call" | custom-call | tf_op jit(solution)/shard_map/finish/pallas_call | solution.py:382
  201.7 11.7 %all-to-all-done.3.c = bf16[16,144,128]{2,1,0:T(8,128)(2,1)} async-done(((bf16[16,144,128]{2,1,0:T(8,128)(2,1)}), bf16[16,144,128]{2,1,0:T(8,128)(2,1)}, u32[]{:S(2)}, u32[]{:S(2)}) %all-to-all-start.3) | async-done | bytes 589856 | tf_op jit(solution)/shard_map/all_to_all | solution.py:402
  213.3 4.5 %finish.3 = (bf16[256,1280]{1,0:T(8,128)(2,1)}, f32[80,1280]{1,0:T(8,128)}) custom-call(s32[16]{0:T(128)} %stack.162._.order, bf16[16,144,128]{2,1,0:T(8,128)(2,1)} %all-to-all-done.3.c, bf16[640,1280]{1,0:T(8,128)(2,1)} %bitcast.69, bf16[640,1280]{1,0:T(8,128)(2,1)} %copy-done.5, f32[256,1280]{1,0:T(8,128)} %copy-done.1, ...), custom_call_target="tpu_custom_call", output_to_operand_aliasing={{0}: (5, {})} | custom-call | tf_op jit(solution)/shard_map/finish/pallas_call | solution.py:382
  (50 shorter events, 1.5 us)
Async XLA Ops:
  0.6 7.4 %copy-start.12 = (bf16[1,256,1280]{2,1,0:T(8,128)(2,1)S(1)}, bf16[1,256,1280]{2,1,0:T(8,128)(2,1)}, u32[]{:S(2)}) copy-start(bf16[1,256,1280]{2,1,0:T(8,128)(2,1)} %param.8) | copy-start | bytes 1966084
  1.9 7.6 %collective-permute-start = (bf16[80,640]{1,0:T(8,128)(2,1)S(1)}, bf16[80,640]{1,0:T(8,128)(2,1)S(1)}, u32[]{:S(2)}, u32[]{:S(2)}) collective-permute-start(bf16[80,640]{1,0:T(8,128)(2,1)S(1)} %get-tuple-element.48), channel_id=1, source_target_pairs={{136,0},{128,8},{8,128},{0,136},{137,1},{129,9},{9,129},{1,137},{1... | collective-permute-start | bytes 307208 | tf_op jit(solution)/shard_map/ppermute | solution.py:34
  8.3 2.7 %copy-start.1 = (f32[256,1280]{1,0:T(8,128)}, f32[256,1280]{1,0:T(8,128)S(1)}, u32[]{:S(2)}) copy-start(f32[256,1280]{1,0:T(8,128)S(1)} %get-tuple-element.41.w_ref.w) | copy-start | bytes 3932164
  8.3 1.1 copy-start.9
  9.6 18.7 %collective-permute-start.1 = (bf16[80,2560]{1,0:T(8,128)(2,1)S(1)}, bf16[80,2560]{1,0:T(8,128)(2,1)S(1)}, u32[]{:S(2)}, u32[]{:S(2)}) collective-permute-start(bf16[80,2560]{1,0:T(8,128)(2,1)S(1)} %pad_maximum_fusion.5), channel_id=1, source_target_pairs={{136,0},{128,8},{8,128},{0,136},{137,1},{129,9},{9,129},{1,137},{1... | collective-permute-start | bytes 1228808 | tf_op jit(solution)/shard_map/ppermute | solution.py:34
  16.5 19.5 %collective-permute-start.9 = (bf16[272,1280]{1,0:T(8,128)(2,1)}, bf16[272,1280]{1,0:T(8,128)(2,1)S(1)}, u32[]{:S(2)}, u32[]{:S(2)}) collective-permute-start(bf16[272,1280]{1,0:T(8,128)(2,1)} %shard_map.95.x_ref), channel_id=1, source_target_pairs={{0,8},{8,0},{1,9},{9,1},{2,10},{10,2},{3,11},{11,3},{4,12},{12,4},... | collective-permute-start | bytes 2088968 | tf_op jit(solution)/shard_map/ppermute | solution.py:30
  16.5 7.6 %collective-permute-start.4 = (bf16[2,80,640]{2,1,0:T(8,128)(2,1)S(1)}, bf16[2,80,640]{2,1,0:T(8,128)(2,1)S(1)}, u32[]{:S(2)}, u32[]{:S(2)}) collective-permute-start(bf16[2,80,640]{2,1,0:T(8,128)(2,1)S(1)} %get-tuple-element.53), channel_id=1, source_target_pairs={{0,96},{32,0},{64,32},{96,64},{1,97},{33,1},{65,33},{97,65},{2,98}... | collective-permute-start | bytes 614408 | tf_op jit(solution)/shard_map/ppermute | solution.py:284
  17.0 8.9 %collective-permute-start.3 = (bf16[2,80,640]{2,1,0:T(8,128)(2,1)S(1)}, bf16[2,80,640]{2,1,0:T(8,128)(2,1)S(1)}, u32[]{:S(2)}, u32[]{:S(2)}) collective-permute-start(bf16[2,80,640]{2,1,0:T(8,128)(2,1)S(1)} %get-tuple-element.53), channel_id=1, source_target_pairs={{0,64},{32,96},{64,0},{96,32},{1,65},{33,97},{65,1},{97,33},{2,66}... | collective-permute-start | bytes 614408 | tf_op jit(solution)/shard_map/ppermute | solution.py:284
  19.7 8.3 %collective-permute-start.2 = (bf16[2,80,640]{2,1,0:T(8,128)(2,1)S(1)}, bf16[2,80,640]{2,1,0:T(8,128)(2,1)S(1)}, u32[]{:S(2)}, u32[]{:S(2)}) collective-permute-start(bf16[2,80,640]{2,1,0:T(8,128)(2,1)S(1)} %get-tuple-element.53), channel_id=1, source_target_pairs={{0,32},{32,64},{64,96},{96,0},{1,33},{33,65},{65,97},{97,1},{2,34}... | collective-permute-start | bytes 614408 | tf_op jit(solution)/shard_map/ppermute | solution.py:284
  28.1 7.8 %copy-start.6 = (bf16[4,2,80,640]{3,2,1,0:T(8,128)(2,1)}, bf16[4,2,80,640]{3,2,1,0:T(8,128)(2,1)S(1)}, u32[]{:S(2)}) copy-start(bf16[4,2,80,640]{3,2,1,0:T(8,128)(2,1)S(1)} %pad_maximum_fusion.3) | copy-start | bytes 2457604
  28.1 7.8 %collective-permute-start.8 = (bf16[640,640]{1,0:T(8,128)(2,1)S(1)}, bf16[640,640]{1,0:T(8,128)(2,1)}, u32[]{:S(2)}, u32[]{:S(2)}) collective-permute-start(bf16[640,640]{1,0:T(8,128)(2,1)S(1)} %bitcast.72), channel_id=1, source_target_pairs={{0,16},{16,0},{1,17},{17,1},{2,18},{18,2},{3,19},{19,3},{4,20},{20... | collective-permute-start | bytes 2457608 | tf_op jit(solution)/shard_map/ppermute | solution.py:26
  29.1 12.5 %collective-permute-start.7 = (bf16[2,80,1280]{2,1,0:T(8,128)(2,1)S(1)}, bf16[2,80,1280]{2,1,0:T(8,128)(2,1)S(1)}, u32[]{:S(2)}, u32[]{:S(2)}) collective-permute-start(bf16[2,80,1280]{2,1,0:T(8,128)(2,1)S(1)} %pad_maximum_fusion.6), channel_id=1, source_target_pairs={{0,96},{32,0},{64,32},{96,64},{1,97},{33,1},{65,33},{97,65},{2,98}... | collective-permute-start | bytes 1228808 | tf_op jit(solution)/shard_map/ppermute | solution.py:284
  29.8 13.9 %collective-permute-start.6 = (bf16[2,80,1280]{2,1,0:T(8,128)(2,1)S(1)}, bf16[2,80,1280]{2,1,0:T(8,128)(2,1)S(1)}, u32[]{:S(2)}, u32[]{:S(2)}) collective-permute-start(bf16[2,80,1280]{2,1,0:T(8,128)(2,1)S(1)} %pad_maximum_fusion.6), channel_id=1, source_target_pairs={{0,64},{32,96},{64,0},{96,32},{1,65},{33,97},{65,1},{97,33},{2,66}... | collective-permute-start | bytes 1228808 | tf_op jit(solution)/shard_map/ppermute | solution.py:284
  32.6 19.0 %collective-permute-start.5 = (bf16[2,80,1280]{2,1,0:T(8,128)(2,1)S(1)}, bf16[2,80,1280]{2,1,0:T(8,128)(2,1)}, u32[]{:S(2)}, u32[]{:S(2)}) collective-permute-start(bf16[2,80,1280]{2,1,0:T(8,128)(2,1)S(1)} %pad_maximum_fusion.6), channel_id=1, source_target_pairs={{0,32},{32,64},{64,96},{96,0},{1,33},{33,65},{65,97},{97,1},{2,34}... | collective-permute-start | bytes 1228808 | tf_op jit(solution)/shard_map/ppermute | solution.py:284
  35.9 0.9 copy-start.7
  51.6 1.6 copy-start.11
  52.9 1.2 copy-start.4
  52.9 20.7 %collective-permute-start.10 = (bf16[640,1280]{1,0:T(8,128)(2,1)S(1)}, bf16[640,1280]{1,0:T(8,128)(2,1)}, u32[]{:S(2)}, u32[]{:S(2)}) collective-permute-start(bf16[640,1280]{1,0:T(8,128)(2,1)S(1)} %bitcast.70), channel_id=1, source_target_pairs={{0,16},{16,0},{1,17},{17,1},{2,18},{18,2},{3,19},{19,3},{4,20},{20... | collective-permute-start | bytes 4915208 | tf_op jit(solution)/shard_map/ppermute | solution.py:26
  54.1 31.8 %all-to-all-start.1 = ((bf16[8,96,512]{2,1,0:T(8,128)(2,1)}), bf16[8,96,512]{2,1,0:T(8,128)(2,1)S(1)}, u32[]{:S(2)}, u32[]{:S(2)}) async-start(bf16[8,96,512]{2,1,0:T(8,128)(2,1)} %shard_map.96), calls=%async_computation.1 | async-start | bytes 1572864 | tf_op jit(solution)/shard_map/all_to_all | solution.py:326
  64.8 3.4 %collective-permute-start.11 = (bf16[512,1280]{1,0:T(8,128)(2,1)}, bf16[512,1280]{1,0:T(8,128)(2,1)}, u32[]{:S(2)}, u32[]{:S(2)}) collective-permute-start(bf16[512,1280]{1,0:T(8,128)(2,1)} %pad_maximum_fusion.2.refs_0_), channel_id=1, source_target_pairs={{0,16},{16,0},{1,17},{17,1},{2,18},{18,2},{3,19},{19,3},{4,20},{20... | collective-permute-start | bytes 3932168 | tf_op jit(solution)/shard_map/ppermute | solution.py:26
  80.0 32.8 %copy-start.8 = (f32[2,80,1280]{2,1,0:T(8,128)S(1)}, f32[2,80,1280]{2,1,0:T(8,128)}, u32[]{:S(2)}) copy-start(f32[2,80,1280]{2,1,0:T(8,128)} %get-tuple-element.28) | copy-start | bytes 2457604
  85.8 0.9 copy-start.3
  86.7 41.9 %all-to-all-start = ((bf16[8,160,512]{2,1,0:T(8,128)(2,1)}), bf16[8,160,512]{2,1,0:T(8,128)(2,1)S(1)}, u32[]{:S(2)}, u32[]{:S(2)}) async-start(bf16[8,160,512]{2,1,0:T(8,128)(2,1)} %shard_map.98), calls=%async_computation | async-start | bytes 2621440 | tf_op jit(solution)/shard_map/all_to_all | solution.py:344
  90.3 11.7 %collective-permute-start.12 = (bf16[2,80,1280]{2,1,0:T(8,128)(2,1)}, bf16[2,80,1280]{2,1,0:T(8,128)(2,1)S(1)}, u32[]{:S(2)}, u32[]{:S(2)}) collective-permute-start(bf16[2,80,1280]{2,1,0:T(8,128)(2,1)} %get-tuple-element.33), channel_id=1, source_target_pairs={{0,32},{32,64},{64,96},{96,0},{1,33},{33,65},{65,97},{97,1},{2,34}... | collective-permute-start | bytes 1228808 | tf_op jit(solution)/shard_map/ppermute | solution.py:284
  91.6 20.2 %collective-permute-start.13 = (bf16[2,80,1280]{2,1,0:T(8,128)(2,1)}, bf16[2,80,1280]{2,1,0:T(8,128)(2,1)S(1)}, u32[]{:S(2)}, u32[]{:S(2)}) collective-permute-start(bf16[2,80,1280]{2,1,0:T(8,128)(2,1)} %get-tuple-element.34), channel_id=1, source_target_pairs={{0,64},{32,96},{64,0},{96,32},{1,65},{33,97},{65,1},{97,33},{2,66}... | collective-permute-start | bytes 1228808 | tf_op jit(solution)/shard_map/ppermute | solution.py:284
  93.3 19.5 %collective-permute-start.14 = (bf16[2,80,1280]{2,1,0:T(8,128)(2,1)}, bf16[2,80,1280]{2,1,0:T(8,128)(2,1)S(1)}, u32[]{:S(2)}, u32[]{:S(2)}) collective-permute-start(bf16[2,80,1280]{2,1,0:T(8,128)(2,1)} %get-tuple-element.35), channel_id=1, source_target_pairs={{0,96},{32,0},{64,32},{96,64},{1,97},{33,1},{65,33},{97,65},{2,98}... | collective-permute-start | bytes 1228808 | tf_op jit(solution)/shard_map/ppermute | solution.py:284
  112.9 3.6 %copy-start.10 = (bf16[1,80,1280]{2,1,0:T(8,128)(2,1)S(1)}, bf16[1,80,1280]{2,1,0:T(8,128)(2,1)}, u32[]{:S(2)}) copy-start(bf16[1,80,1280]{2,1,0:T(8,128)(2,1)} %get-tuple-element.50) | copy-start | bytes 614404
  113.7 11.6 %collective-permute-start.15 = (f32[80,1280]{1,0:T(8,128)S(1)}, f32[80,1280]{1,0:T(8,128)S(1)}, u32[]{:S(2)}, u32[]{:S(2)}) collective-permute-start(f32[80,1280]{1,0:T(8,128)S(1)} %get-tuple-element.42), channel_id=1, source_target_pairs={{136,0},{128,8},{8,128},{0,136},{137,1},{129,9},{9,129},{1,137},{1... | collective-permute-start | bytes 1228808 | tf_op jit(solution)/shard_map/ppermute | solution.py:34
  125.4 0.8 copy-start.13
  128.7 1.1 copy-start
  142.1 43.3 %all-to-all-start.2 = ((bf16[16,144,128]{2,1,0:T(8,128)(2,1)}), bf16[16,144,128]{2,1,0:T(8,128)(2,1)}, u32[]{:S(2)}, u32[]{:S(2)}) async-start(bf16[16,144,128]{2,1,0:T(8,128)(2,1)} %bitcast.75), calls=%async_computation.2 | async-start | bytes 1179648 | tf_op jit(solution)/shard_map/all_to_all | solution.py:398
  149.4 14.0 %collective-permute-start.18 = (bf16[2,80,1280]{2,1,0:T(8,128)(2,1)S(1)}, bf16[2,80,1280]{2,1,0:T(8,128)(2,1)S(1)}, u32[]{:S(2)}, u32[]{:S(2)}) collective-permute-start(bf16[2,80,1280]{2,1,0:T(8,128)(2,1)S(1)} %pad_maximum_fusion.7), channel_id=1, source_target_pairs={{0,96},{32,0},{64,32},{96,64},{1,97},{33,1},{65,33},{97,65},{2,98}... | collective-permute-start | bytes 1228808 | tf_op jit(solution)/shard_map/ppermute | solution.py:284
  151.9 13.9 %collective-permute-start.17 = (bf16[2,80,1280]{2,1,0:T(8,128)(2,1)S(1)}, bf16[2,80,1280]{2,1,0:T(8,128)(2,1)S(1)}, u32[]{:S(2)}, u32[]{:S(2)}) collective-permute-start(bf16[2,80,1280]{2,1,0:T(8,128)(2,1)S(1)} %pad_maximum_fusion.7), channel_id=1, source_target_pairs={{0,64},{32,96},{64,0},{96,32},{1,65},{33,97},{65,1},{97,33},{2,66}... | collective-permute-start | bytes 1228808 | tf_op jit(solution)/shard_map/ppermute | solution.py:284
  155.1 17.3 %collective-permute-start.16 = (bf16[2,80,1280]{2,1,0:T(8,128)(2,1)S(1)}, bf16[2,80,1280]{2,1,0:T(8,128)(2,1)S(1)}, u32[]{:S(2)}, u32[]{:S(2)}) collective-permute-start(bf16[2,80,1280]{2,1,0:T(8,128)(2,1)S(1)} %pad_maximum_fusion.7), channel_id=1, source_target_pairs={{0,32},{32,64},{64,96},{96,0},{1,33},{33,65},{65,97},{97,1},{2,34}... | collective-permute-start | bytes 1228808 | tf_op jit(solution)/shard_map/ppermute | solution.py:284
  172.6 12.8 %copy-start.2 = (bf16[4,2,80,1280]{3,2,1,0:T(8,128)(2,1)}, bf16[4,2,80,1280]{3,2,1,0:T(8,128)(2,1)S(1)}, u32[]{:S(2)}) copy-start(bf16[4,2,80,1280]{3,2,1,0:T(8,128)(2,1)S(1)} %pad_maximum_fusion.1) | copy-start | bytes 4915204
  172.6 23.5 %collective-permute-start.19 = (bf16[640,1280]{1,0:T(8,128)(2,1)S(1)}, bf16[640,1280]{1,0:T(8,128)(2,1)S(1)}, u32[]{:S(2)}, u32[]{:S(2)}) collective-permute-start(bf16[640,1280]{1,0:T(8,128)(2,1)S(1)} %bitcast.67), channel_id=1, source_target_pairs={{0,16},{16,0},{1,17},{17,1},{2,18},{18,2},{3,19},{19,3},{4,20},{20... | collective-permute-start | bytes 4915208 | tf_op jit(solution)/shard_map/ppermute | solution.py:26
  188.3 25.0 %all-to-all-start.3 = ((bf16[16,144,128]{2,1,0:T(8,128)(2,1)}), bf16[16,144,128]{2,1,0:T(8,128)(2,1)}, u32[]{:S(2)}, u32[]{:S(2)}) async-start(bf16[16,144,128]{2,1,0:T(8,128)(2,1)} %pad_maximum_fusion.4), calls=%async_computation.3 | async-start | bytes 1179648 | tf_op jit(solution)/shard_map/all_to_all | solution.py:402
  196.1 1.2 copy-start.5
